TPU v7x, 512 devices: a whole 4x4x16 slice. The times are simulated.
512 devices in a mesh: row: 16 (over y_hi, x, core), col: 32 (over z, y_lo).
Axes of the slice: x: 4, y: 4 (y_hi: 2, y_lo: 2; y = y_hi * 2 + y_lo), z: 16, core: 2. Of those that a mesh axis runs over, the one named last changes fastest.
Arguments:
- specimen: float32 [2, 2048, 8192], P(None, 'row', 'col'), may hold values from -6 to 6
- probe_field: float32 [2, 256, 256], replicated, may hold values from -6 to 6
- scan_offsets: int32 [16, 32, 2, 2], replicated, may hold values from -128 to 128, as said below
- live_counts: int32 [16, 32], replicated, may hold values from 1 to 2, as said below
- magnitudes: float32 [16, 32, 2, 256, 256], P('row', 'col'), may hold values from 0 to 2
Outputs:
- specimen_next: float32 [2, 2048, 8192], P(None, 'row', 'col')
- probe_next: float32 [2, 256, 256], replicated
Inputs may be any that keep to these rules, and one draw needn't show every extreme that they name: `scan_offsets`: rows of a patch start within -128 to 0 of the tile's first row, columns within -128 to 128 of its first column. Tile (a, b) owns the positions in its first live_counts[a, b] slots.
All inputs are finite; a program needn't handle non-finite values.
Results may differ from a plain program's by a relative error of at most 0.0003.
Values sent between devices are 32-bit elements; how exact they have to be, the bound alone decides.
A program may use at most 64 MiB of HBM per device.

v0:
```python
import math
import jax
import jax.numpy as jnp
from jax import lax
from jax.sharding import PartitionSpec as P

modulus_floor = 0.25
object_damping = 0.1
probe_damping = 0.1


def extended_2(block, sides, width):
    for axis, dim in sides:
        count = lax.axis_size(axis)
        forward = [(i, i + 1) for i in range(count - 1)]
        backward = [(target, source) for source, target in forward]
        low = lax.ppermute(
            lax.slice_in_dim(block, block.shape[dim] - width, None, axis=dim), axis, forward
        )
        high = lax.ppermute(lax.slice_in_dim(block, 0, width, axis=dim), axis, backward)
        block = jnp.concatenate([low, block, high], axis=dim)
    return block


def dft_tables(width):
    counter = jnp.arange(width, dtype=jnp.int32)
    phase = counter[:, None] * counter[None, :] % width
    angle = phase.astype(jnp.float32) * (2.0 * math.pi / width)
    factor = 1.0 / math.sqrt(width)
    return (jnp.cos(angle) * factor, jnp.sin(angle) * factor)


def matmul_right(left, table):
    return jnp.einsum("sjm,ml->sjl", left, table, precision=lax.Precision.HIGHEST)


def matmul_left(table, right):
    return jnp.einsum("kj,sjl->skl", table, right, precision=lax.Precision.HIGHEST)


def transform(wave_real, wave_imag, cosine, sine, direction):
    inner_real = matmul_right(wave_real, cosine) + direction * matmul_right(wave_imag, sine)
    inner_imag = matmul_right(wave_imag, cosine) - direction * matmul_right(wave_real, sine)
    outer_real = matmul_left(cosine, inner_real) + direction * matmul_left(sine, inner_imag)
    outer_imag = matmul_left(cosine, inner_imag) - direction * matmul_left(sine, inner_real)
    return (outer_real, outer_imag)


def fold_rims(wide, tile_r, tile_c, half):
    center = wide[:, 2 * half : 2 * half + tile_r, :]
    center = center.at[:, :half, :].add(wide[:, :half, :])
    center = center.at[:, tile_r - half :, :].add(wide[:, tile_r + 3 * half :, :])
    result = center[:, :, 2 * half : 2 * half + tile_c]
    result = result.at[:, :, :half].add(center[:, :, :half])
    result = result.at[:, :, tile_c - half :].add(center[:, :, tile_c + 3 * half :])
    return result


def shards(specimen, probe_field, scan_offsets, live_counts, magnitudes):
    width = probe_field.shape[1]
    half = width // 2
    tile_r = specimen.shape[1]
    tile_c = specimen.shape[2]
    slots = magnitudes.shape[2]
    row_place = lax.axis_index("row")
    col_place = lax.axis_index("col")
    zero_index = jnp.zeros((), jnp.int32)
    extended = extended_2(specimen, (("row", 1), ("col", 2)), half)
    offsets_here = scan_offsets[row_place, col_place]
    live = (jnp.arange(slots, dtype=jnp.int32) < live_counts[row_place, col_place]).astype(
        jnp.float32
    )[:, None, None]
    row_starts = offsets_here[:, 0] + half
    col_starts = offsets_here[:, 1] + half

    def extract(row_start, col_start):
        return lax.dynamic_slice(extended, (zero_index, row_start, col_start), (2, width, width))

    patches = jax.vmap(extract)(row_starts, col_starts)
    patch_real = patches[:, 0]
    patch_imag = patches[:, 1]
    probe_real = probe_field[0]
    probe_imag = probe_field[1]
    power = probe_real * probe_real + probe_imag * probe_imag
    cosine, sine = dft_tables(width)
    wave_real = probe_real * patch_real - probe_imag * patch_imag
    wave_imag = probe_real * patch_imag + probe_imag * patch_real
    far_real, far_imag = transform(wave_real, wave_imag, cosine, sine, 1.0)
    modulus = jnp.sqrt(far_real * far_real + far_imag * far_imag)
    factor = magnitudes[0, 0] / jnp.maximum(modulus, modulus_floor) - 1.0
    diff_real, diff_imag = transform(far_real * factor, far_imag * factor, cosine, sine, -1.0)
    diff_real = diff_real * live
    diff_imag = diff_imag * live
    grad_real = probe_real * diff_real + probe_imag * diff_imag
    grad_imag = probe_real * diff_imag - probe_imag * diff_real
    pieces = jnp.stack([grad_real, grad_imag, live * power], axis=1)
    layers = pieces.shape[1]

    def place(slot, total):
        start = (zero_index, row_starts[slot], col_starts[slot])
        current = lax.dynamic_slice(total, start, (layers, width, width))
        return lax.dynamic_update_slice(total, current + pieces[slot], start)

    start_total = jnp.zeros((layers, tile_r + 2 * half, tile_c + 2 * half), jnp.float32)
    buffer = lax.fori_loop(0, slots, place, start_total)
    wide = extended_2(buffer, (("row", 1), ("col", 2)), half)
    folded = fold_rims(wide, tile_r, tile_c, half)
    update = folded[:2]
    lighting = folded[2]
    damping = object_damping * jnp.max(power)
    specimen_next = specimen + update / (lighting + damping)
    local_terms = (
        jnp.sum(patch_real * diff_real + patch_imag * diff_imag, 0),
        jnp.sum(patch_real * diff_imag - patch_imag * diff_real, 0),
        jnp.sum(live * (patch_real * patch_real + patch_imag * patch_imag), 0),
    )
    sum_real, sum_imag, weight = lax.psum(
        (local_terms[0], local_terms[1], local_terms[2]), ("row", "col")
    )
    denominator = weight + probe_damping * jnp.mean(weight)
    probe_next = probe_field + jnp.stack([sum_real, sum_imag]) / denominator
    return (specimen_next, probe_next)


def solution(mesh):
    return jax.shard_map(
        shards,
        mesh=mesh,
        in_specs=(P(None, "row", "col"), P(), P(), P(), P("row", "col", None, None, None)),
        out_specs=(P(None, "row", "col"), P()),
        check_vma=False,
    )
```

profile of v0, /device:TPU:8, one launch (start us, length us, event | category | flops | bytes accessed | tf_op | source)
XLA Modules:
  0.0 654.2 jit_solution(3833202811847272772)
XLA Ops:
  7.2 1.9 collective-permute-start
  15.0 3.7 collective-permute-start.2
  18.7 4.1 collective-permute-start.3
  24.7 13.0 %collective-permute-done.2 = f32[2,384,128]{2,1,0:T(8,128)S(1)} collective-permute-done((f32[2,384,128]{2,1,0:T(8,128)}, f32[2,384,128]{2,1,0:T(8,128)S(1)}, u32[]{:S(2)}, u32[]{:S(2)}) %collective-permute-start.2) | collective-permute-done | bytes 393248 | tf_op jit(solution)/shard_map/ppermute | solution.py:17
  39.7 5.8 while.21
  40.4 2.3 bitcast_dynamic-update-slice_fusion.2
  43.3 2.2 bitcast_dynamic-update-slice_fusion.2
  45.6 2.9 fusion.49
  55.1 1.8 fusion.51
  56.9 2.0 fusion.8
  58.9 2.0 fusion.25
  69.1 2.6 fusion.39
  71.7 2.4 fusion.4
  75.3 4.0 fusion.16
  80.8 34.3 %while.20 = (s32[]{:T(128)}, f32[3,384,512]{2,1,0:T(8,128)S(1)}, s32[2]{0:T(128)S(1)}, s32[2]{0:T(128)S(1)}, f32[2,3,256,256]{3,2,0,1:T(8,128)}, /*index=5*/s32[]{:T(128)}, s32[]{:T(128)}, s32[]{:T(128)}, s32[]{:T(128)}) while((s32[]{:T(128)}, f32[3,384,512]{2,1,0:T(8,128)S(1)}, s32[2]{0:T(128)S(1)}, s32[2]{0:T(128)S(1)}, ...), condition=%wide.region_1.2_spmd, body=%wide.region_0.1_spmd.sunk | while | flops 196616 | bytes 3932361 | solution.py:105
  87.4 10.8 %dynamic_update_slice.8 = f32[3,384,512]{2,1,0:T(8,128)S(1)} dynamic-update-slice(f32[3,384,512]{2,1,0:T(8,128)S(1)} %get-tuple-element.311, f32[3,256,256]{2,1,0:T(8,128)S(1)} %bitcast_add_fusion.2, s32[]{:T(128)} %constant.194.clone.1..sunk, s32[]{:T(128)S(6)} %select_n.146, s32[]{:T(128)S(6)} %select_n.147) | dynamic-update-slice | bytes 1572868 | tf_op jit(solution)/shard_map/while/body/eval_jaxpr/dynamic_update_slice | solution.py:102
  104.8 10.4 %dynamic_update_slice.8 = f32[3,384,512]{2,1,0:T(8,128)S(1)} dynamic-update-slice(f32[3,384,512]{2,1,0:T(8,128)S(1)} %get-tuple-element.311, f32[3,256,256]{2,1,0:T(8,128)S(1)} %bitcast_add_fusion.2, s32[]{:T(128)} %constant.194.clone.1..sunk, s32[]{:T(128)S(6)} %select_n.146, s32[]{:T(128)S(6)} %select_n.147) | dynamic-update-slice | bytes 1572868 | tf_op jit(solution)/shard_map/while/body/eval_jaxpr/dynamic_update_slice | solution.py:102
  115.3 8.6 %collective-permute-start.4 = (f32[3,128,512]{2,1,0:T(8,128)S(1)}, f32[3,128,512]{2,1,0:T(8,128)S(1)}, u32[]{:S(2)}, u32[]{:S(2)}) collective-permute-start(f32[3,128,512]{2,1,0:T(8,128)S(1)} %get-tuple-element.210), channel_id=1, source_target_pairs={{0,32},{32,64},{64,96},{96,128},{128,160},{160,192},{192,224},{224... | collective-permute-start | bytes 2359304 | tf_op jit(solution)/shard_map/ppermute | solution.py:17
  126.1 3.6 collective-permute-done.5
  131.9 2.4 collective-permute-start.6
  134.3 3.5 collective-permute-start.7
  139.3 498.2 %all-reduce.3.cloned.1.call-done = (f32[1,256,256]{2,1,0:T(8,128)}, f32[1,256,256]{2,1,0:T(8,128)}, f32[256,256]{1,0:T(8,128)}) async-done(((f32[1,256,256]{2,1,0:T(8,128)}, f32[1,256,256]{2,1,0:T(8,128)}, f32[256,256]{1,0:T(8,128)}), (f32[1,256,256]{2,1,0:T(8,128)}, f32[1,256,256]{2,1,0:T(8,128)}, f32[256,256]{1,0:T(8,128)})) %all-reduce.3.cloned.1.call-update) | async-done | bytes 786448 | tf_op jit(solution)/shard_map/psum | solution.py:117
  640.8 1.9 fusion.10
  642.7 1.9 fusion.9
  (80 shorter events, 44.6 us)
Async XLA Ops:
  7.2 4.4 copy-start
  7.2 6.1 copy-start.5
  7.2 630.3 %all-reduce.3.cloned.1.call-start = ((), (), s32[]{:S(2)}) async-start(), calls=%async_computation | async-start | bytes 1572864 | tf_op jit(solution)/shard_map/psum | solution.py:117
  7.2 6.0 collective-permute-start
  9.1 4.9 collective-permute-start.1
  13.2 10.3 %copy-start.7 = (f32[1,1,2,256,256]{4,3,2,1,0:T(8,128)S(1)}, f32[1,1,2,256,256]{4,3,2,1,0:T(8,128)}, u32[]{:S(2)}) copy-start(f32[1,1,2,256,256]{4,3,2,1,0:T(8,128)} %param.23) | copy-start | bytes 1572868
  15.0 22.7 %collective-permute-start.2 = (f32[2,384,128]{2,1,0:T(8,128)}, f32[2,384,128]{2,1,0:T(8,128)S(1)}, u32[]{:S(2)}, u32[]{:S(2)}) collective-permute-start(f32[2,384,128]{2,1,0:T(8,128)} %get-tuple-element.217), channel_id=1, source_target_pairs={{0,1},{1,2},{2,3},{3,4},{4,5},{5,6},{6,7},{7,8},{8,9},{9,10},{10,1... | collective-permute-start | bytes 1179656 | tf_op jit(solution)/shard_map/ppermute | solution.py:17
  18.7 19.7 %collective-permute-start.3 = (f32[2,384,128]{2,1,0:T(8,128)}, f32[2,384,128]{2,1,0:T(8,128)}, u32[]{:S(2)}, u32[]{:S(2)}) collective-permute-start(f32[2,384,128]{2,1,0:T(8,128)} %get-tuple-element.218), channel_id=1, source_target_pairs={{1,0},{2,1},{3,2},{4,3},{5,4},{6,5},{7,6},{8,7},{9,8},{10,9},{11,1... | collective-permute-start | bytes 1179656 | tf_op jit(solution)/shard_map/ppermute | solution.py:20
  37.7 0.8 copy-start.9
  45.6 2.9 copy-start.4
  55.1 3.8 copy-start.8
  115.3 10.5 %collective-permute-start.4 = (f32[3,128,512]{2,1,0:T(8,128)S(1)}, f32[3,128,512]{2,1,0:T(8,128)S(1)}, u32[]{:S(2)}, u32[]{:S(2)}) collective-permute-start(f32[3,128,512]{2,1,0:T(8,128)S(1)} %get-tuple-element.210), channel_id=1, source_target_pairs={{0,32},{32,64},{64,96},{96,128},{128,160},{160,192},{192,224},{224... | collective-permute-start | bytes 2359304 | tf_op jit(solution)/shard_map/ppermute | solution.py:17
  124.0 5.7 collective-permute-start.5
  129.7 2.2 copy-start.1
  129.7 8.1 %copy-start.3 = (f32[2,256,256]{2,1,0:T(8,128)S(1)}, f32[2,256,256]{2,1,0:T(8,128)}, u32[]{:S(2)}) copy-start(f32[2,256,256]{2,1,0:T(8,128)} %param.20) | copy-start | bytes 1572868
  131.9 510.8 %collective-permute-start.6 = (f32[3,640,128]{2,1,0:T(8,128)}, f32[3,640,128]{2,1,0:T(8,128)S(1)}, u32[]{:S(2)}, u32[]{:S(2)}) collective-permute-start(f32[3,640,128]{2,1,0:T(8,128)} %get-tuple-element.207), channel_id=1, source_target_pairs={{0,1},{1,2},{2,3},{3,4},{4,5},{5,6},{6,7},{7,8},{8,9},{9,10},{10,1... | collective-permute-start | bytes 2949128 | tf_op jit(solution)/shard_map/ppermute | solution.py:17
  134.3 508.4 %collective-permute-start.7 = (f32[3,640,128]{2,1,0:T(8,128)S(1)}, f32[3,640,128]{2,1,0:T(8,128)S(1)}, u32[]{:S(2)}, u32[]{:S(2)}) collective-permute-start(f32[3,640,128]{2,1,0:T(8,128)S(1)} %get-tuple-element.208), channel_id=1, source_target_pairs={{1,0},{2,1},{3,2},{4,3},{5,4},{6,5},{7,6},{8,7},{9,8},{10,9},{11,1... | collective-permute-start | bytes 2949128 | tf_op jit(solution)/shard_map/ppermute | solution.py:20
  642.7 2.8 copy-start.2
  645.6 1.0 copy-start.6
Sparse Core Ops, SparseCore 0:
  138.0 499.5 all-reduce.2
where the time goes:
time: 655 us; the launch traced here: 654 us
  waiting for transfers between devices  516 us (79%)
  local copies, waits for them, and re-layouts  39.8 us (6%)
  matrix products  32.3 us (5%)
  starting transfers between devices  26.8 us (4%)
  between operations  15.8 us (2%)
  other arithmetic  15.6 us (2%)
  loops' own time  7.67 us (1%)
    psum x1, waiting for transfers between devices, shards(): lax.psum((local_terms[0], local_terms[1], local_terms[2]), ('row', 'col'))  498 us
    dynamic_update_slice x2, local copies, waits for them, and re-layouts, place(): return lax.dynamic_update_slice(total, current + pieces[slot], start)  21.2 us
    dot_general x8, matrix products, matmul_left(): jnp.einsum('kj,sjl->skl', table, right, precision=lax.Precision.HIGHEST)  18.1 us
    ppermute x4, starting transfers between devices, extended_2(): lax.ppermute(lax.slice_in_dim(block, block.shape[dim] - width, None, axis...  16.6 us
    dot_general x8, matrix products, matmul_right(): jnp.einsum('sjm,ml->sjl', left, table, precision=lax.Precision.HIGHEST)  14.2 us
    ppermute x4, waiting for transfers between devices, extended_2(): lax.ppermute(lax.slice_in_dim(block, block.shape[dim] - width, None, axis...  13.5 us
  transfers between devices with their start and end apart: 9, of which 5 were waited for; matrix products, arithmetic and copies ran while one was open for 2% of the time, Pallas kernels for 0%

commit v1 on v0

--- a/solution.py
+++ b/solution.py
@@ -115,7 +115,7 @@
         jnp.sum(live * (patch_real * patch_real + patch_imag * patch_imag), 0),
     )
     sum_real, sum_imag, weight = lax.psum(
-        (local_terms[0], local_terms[1], local_terms[2]), ("row", "col")
+        lax.psum((local_terms[0], local_terms[1], local_terms[2]), "col"), "row"
     )
     denominator = weight + probe_damping * jnp.mean(weight)
     probe_next = probe_field + jnp.stack([sum_real, sum_imag]) / denominator

time: 655 us -> 580 us (0.89)
  the two profiles are of different devices: /device:TPU:8 before, /device:TPU:1 now
where the time goes in v1:
time: 580 us; the launch traced here: 579 us
  waiting for transfers between devices  439 us (76%)
  local copies, waits for them, and re-layouts  46.1 us (8%)
  matrix products  32.4 us (6%)
  starting transfers between devices  22.1 us (4%)
  between operations  15.8 us (3%)
  other arithmetic  15.5 us (3%)
  loops' own time  8.34 us (1%)
    psum x1, waiting for transfers between devices, shards(): lax.psum((local_terms[0], local_terms[1], local_terms[2]), 'col')  246 us
    psum x1, waiting for transfers between devices, shards(): lax.psum(lax.psum((local_terms[0], local_terms[1], local_terms[2]), 'col'...  181 us
    dynamic_update_slice x2, local copies, waits for them, and re-layouts, place(): return lax.dynamic_update_slice(total, current + pieces[slot], start)  25.3 us
    dot_general x8, matrix products, matmul_left(): jnp.einsum('kj,sjl->skl', table, right, precision=lax.Precision.HIGHEST)  18.1 us
    dot_general x8, matrix products, matmul_right(): jnp.einsum('sjm,ml->sjl', left, table, precision=lax.Precision.HIGHEST)  14.3 us
    ppermute x4, waiting for transfers between devices, extended_2(): lax.ppermute(lax.slice_in_dim(block, block.shape[dim] - width, None, axis...  12.7 us
  transfers between devices with their start and end apart: 10, of which 3 were waited for; matrix products, arithmetic and copies ran while one was open for 2% of the time, Pallas kernels for 0%

profile of v1, /device:TPU:1, one launch (start us, length us, event | category | flops | bytes accessed | tf_op | source)
XLA Modules:
  0.0 579.4 jit_solution(15719513567809880462)
XLA Ops:
  7.2 4.6 collective-permute-start
  11.9 5.6 collective-permute-start.1
  21.3 2.7 collective-permute-start.2
  27.2 12.7 %collective-permute-done.2 = f32[2,384,128]{2,1,0:T(8,128)S(1)} collective-permute-done((f32[2,384,128]{2,1,0:T(8,128)}, f32[2,384,128]{2,1,0:T(8,128)S(1)}, u32[]{:S(2)}, u32[]{:S(2)}) %collective-permute-start.2) | collective-permute-done | bytes 393248 | tf_op jit(solution)/shard_map/ppermute | solution.py:17
  41.9 5.7 while.21
  42.5 2.2 bitcast_dynamic-update-slice_fusion.2
  45.4 2.2 bitcast_dynamic-update-slice_fusion.2
  47.6 2.9 fusion.49
  55.3 1.8 fusion.51
  57.1 1.8 fusion.47
  58.9 2.0 fusion.8
  60.9 2.0 fusion.25
  71.1 2.6 fusion.39
  73.8 2.4 fusion.4
  77.4 4.0 fusion.16
  82.9 39.1 %while.20 = (s32[]{:T(128)}, f32[3,384,512]{2,1,0:T(8,128)S(1)}, s32[2]{0:T(128)S(1)}, s32[2]{0:T(128)S(1)}, f32[2,3,256,256]{3,2,0,1:T(8,128)}, /*index=5*/s32[]{:T(128)}, s32[]{:T(128)}, s32[]{:T(128)}, s32[]{:T(128)}) while((s32[]{:T(128)}, f32[3,384,512]{2,1,0:T(8,128)S(1)}, s32[2]{0:T(128)S(1)}, s32[2]{0:T(128)S(1)}, ...), condition=%wide.region_1.2_spmd, body=%wide.region_0.1_spmd.sunk | while | flops 196616 | bytes 3932361 | solution.py:105
  89.8 11.6 %dynamic_update_slice.8 = f32[3,384,512]{2,1,0:T(8,128)S(1)} dynamic-update-slice(f32[3,384,512]{2,1,0:T(8,128)S(1)} %get-tuple-element.314, f32[3,256,256]{2,1,0:T(8,128)S(1)} %bitcast_add_fusion.2, s32[]{:T(128)} %constant.194.clone.1..sunk, s32[]{:T(128)S(6)} %select_n.146, s32[]{:T(128)S(6)} %select_n.147) | dynamic-update-slice | bytes 1572868 | tf_op jit(solution)/shard_map/while/body/eval_jaxpr/dynamic_update_slice | solution.py:102
  108.4 13.6 %dynamic_update_slice.8 = f32[3,384,512]{2,1,0:T(8,128)S(1)} dynamic-update-slice(f32[3,384,512]{2,1,0:T(8,128)S(1)} %get-tuple-element.314, f32[3,256,256]{2,1,0:T(8,128)S(1)} %bitcast_add_fusion.2, s32[]{:T(128)} %constant.194.clone.1..sunk, s32[]{:T(128)S(6)} %select_n.146, s32[]{:T(128)S(6)} %select_n.147) | dynamic-update-slice | bytes 1572868 | tf_op jit(solution)/shard_map/while/body/eval_jaxpr/dynamic_update_slice | solution.py:102
  123.3 1.9 collective-permute-start.4
  125.3 3.3 collective-permute-start.5
  128.5 246.0 %all-reduce.5.cloned.1.call-done = (f32[256,256]{1,0:T(8,128)}, f32[256,256]{1,0:T(8,128)}, f32[256,256]{1,0:T(8,128)}) async-done(((f32[256,256]{1,0:T(8,128)}, f32[256,256]{1,0:T(8,128)}, f32[256,256]{1,0:T(8,128)}), (f32[256,256]{1,0:T(8,128)}, f32[256,256]{1,0:T(8,128)}, f32[256,256]{1,0:T(8,128)})) %all-reduce.5.cloned.1.call-update) | async-done | bytes 786448 | tf_op jit(solution)/shard_map/psum | solution.py:118
  382.3 180.5 %all-reduce.7.cloned.1.call-done = (f32[1,256,256]{2,1,0:T(8,128)}, f32[1,256,256]{2,1,0:T(8,128)}, f32[256,256]{1,0:T(8,128)}) async-done(((f32[1,256,256]{2,1,0:T(8,128)}, f32[1,256,256]{2,1,0:T(8,128)}, f32[256,256]{1,0:T(8,128)}), (f32[1,256,256]{2,1,0:T(8,128)}, f32[1,256,256]{2,1,0:T(8,128)}, f32[256,256]{1,0:T(8,128)})) %all-reduce.7.cloned.1.call-update) | async-done | bytes 786448 | tf_op jit(solution)/shard_map/psum | solution.py:117
  566.1 1.9 fusion.10
  568.0 1.9 fusion.9
  (83 shorter events, 45.1 us)
Async XLA Ops:
  7.2 11.4 %copy-start = (s32[16,32,2,2]{1,3,2,0:T(2,128)S(1)}, s32[16,32,2,2]{1,3,2,0:T(2,128)}, u32[]{:S(2)}) copy-start(s32[16,32,2,2]{1,3,2,0:T(2,128)} %param.21) | copy-start | bytes 24580
  7.2 13.1 %copy-start.5 = (f32[2,128,256]{2,1,0:T(8,128)S(1)}, f32[2,128,256]{2,1,0:T(8,128)}, u32[]{:S(2)}) copy-start(f32[2,128,256]{2,1,0:T(8,128)} %param.19) | copy-start | bytes 786436
  7.2 367.4 %all-reduce.5.cloned.1.call-start = ((), (), s32[]{:S(2)}) async-start(), calls=%async_computation | async-start | bytes 1572864 | tf_op jit(solution)/shard_map/psum | solution.py:118
  7.2 13.0 %collective-permute-start = (f32[2,128,256]{2,1,0:T(8,128)}, f32[2,128,256]{2,1,0:T(8,128)S(1)}, u32[]{:S(2)}, u32[]{:S(2)}) collective-permute-start(f32[2,128,256]{2,1,0:T(8,128)} %param.19), channel_id=1, source_target_pairs={{0,32},{32,64},{64,96},{96,128},{128,160},{160,192},{192,224},{224... | collective-permute-start | bytes 786440 | tf_op jit(solution)/shard_map/ppermute | solution.py:17
  11.9 8.4 %collective-permute-start.1 = (f32[2,128,256]{2,1,0:T(8,128)}, f32[2,128,256]{2,1,0:T(8,128)S(1)}, u32[]{:S(2)}, u32[]{:S(2)}) collective-permute-start(f32[2,128,256]{2,1,0:T(8,128)} %param.19), channel_id=1, source_target_pairs={{32,0},{64,32},{96,64},{128,96},{160,128},{192,160},{224,192},{256... | collective-permute-start | bytes 786440 | tf_op jit(solution)/shard_map/ppermute | solution.py:20
  20.2 5.7 copy-start.7
  21.3 18.5 %collective-permute-start.2 = (f32[2,384,128]{2,1,0:T(8,128)}, f32[2,384,128]{2,1,0:T(8,128)S(1)}, u32[]{:S(2)}, u32[]{:S(2)}) collective-permute-start(f32[2,384,128]{2,1,0:T(8,128)} %get-tuple-element.220), channel_id=1, source_target_pairs={{0,1},{1,2},{2,3},{3,4},{4,5},{5,6},{6,7},{7,8},{8,9},{9,10},{10,1... | collective-permute-start | bytes 1179656 | tf_op jit(solution)/shard_map/ppermute | solution.py:17
  24.0 16.6 %collective-permute-start.3 = (f32[2,384,128]{2,1,0:T(8,128)}, f32[2,384,128]{2,1,0:T(8,128)}, u32[]{:S(2)}, u32[]{:S(2)}) collective-permute-start(f32[2,384,128]{2,1,0:T(8,128)} %get-tuple-element.221), channel_id=1, source_target_pairs={{1,0},{2,1},{3,2},{4,3},{5,4},{6,5},{7,6},{8,7},{9,8},{10,9},{11,1... | collective-permute-start | bytes 1179656 | tf_op jit(solution)/shard_map/ppermute | solution.py:20
  39.8 0.8 copy-start.9
  47.6 2.9 copy-start.4
  57.1 3.8 copy-start.8
  122.0 440.8 %all-reduce.7.cloned.1.call-start = ((), (), s32[]{:S(2)}) async-start(), calls=%async_computation.1 | async-start | bytes 1572864 | tf_op jit(solution)/shard_map/psum | solution.py:117
  123.3 251.2 %collective-permute-start.4 = (f32[3,128,512]{2,1,0:T(8,128)}, f32[3,128,512]{2,1,0:T(8,128)}, u32[]{:S(2)}, u32[]{:S(2)}) collective-permute-start(f32[3,128,512]{2,1,0:T(8,128)} %get-tuple-element.213), channel_id=1, source_target_pairs={{0,32},{32,64},{64,96},{96,128},{128,160},{160,192},{192,224},{224... | collective-permute-start | bytes 2359304 | tf_op jit(solution)/shard_map/ppermute | solution.py:17
  125.3 250.7 %collective-permute-start.5 = (f32[3,128,512]{2,1,0:T(8,128)}, f32[3,128,512]{2,1,0:T(8,128)S(1)}, u32[]{:S(2)}, u32[]{:S(2)}) collective-permute-start(f32[3,128,512]{2,1,0:T(8,128)} %get-tuple-element.212), channel_id=1, source_target_pairs={{32,0},{64,32},{96,64},{128,96},{160,128},{192,160},{224,192},{256... | collective-permute-start | bytes 2359304 | tf_op jit(solution)/shard_map/ppermute | solution.py:20
  376.1 2.2 copy-start.1
  376.1 4.9 copy-start.3
  378.3 189.7 %collective-permute-start.6 = (f32[3,640,128]{2,1,0:T(8,128)}, f32[3,640,128]{2,1,0:T(8,128)S(1)}, u32[]{:S(2)}, u32[]{:S(2)}) collective-permute-start(f32[3,640,128]{2,1,0:T(8,128)} %get-tuple-element.210), channel_id=1, source_target_pairs={{0,1},{1,2},{2,3},{3,4},{4,5},{5,6},{6,7},{7,8},{8,9},{9,10},{10,1... | collective-permute-start | bytes 2949128 | tf_op jit(solution)/shard_map/ppermute | solution.py:17
  379.6 188.3 %collective-permute-start.7 = (f32[3,640,128]{2,1,0:T(8,128)S(1)}, f32[3,640,128]{2,1,0:T(8,128)S(1)}, u32[]{:S(2)}, u32[]{:S(2)}) collective-permute-start(f32[3,640,128]{2,1,0:T(8,128)S(1)} %get-tuple-element.211), channel_id=1, source_target_pairs={{1,0},{2,1},{3,2},{4,3},{5,4},{6,5},{7,6},{8,7},{9,8},{10,9},{11,1... | collective-permute-start | bytes 2949128 | tf_op jit(solution)/shard_map/ppermute | solution.py:20
  568.0 2.8 copy-start.2
  570.9 1.0 copy-start.6
Sparse Core Ops, SparseCore 0:
  122.1 252.3 all-reduce.4
  377.7 185.0 all-reduce.6
